TPU v7x, 256 devices: a whole 4x4x8 slice. The times are simulated.
256 devices in a mesh: ctx: 32 (over y_hi, z, core), tp: 8 (over y_lo, x).
Axes of the slice: x: 4, y: 4 (y_hi: 2, y_lo: 2; y = y_hi * 2 + y_lo), z: 8, core: 2. Of those that a mesh axis runs over, the one named last changes fastest.
Arguments:
- tokens: bfloat16 [8192, 8192], P(('ctx', 'tp')), may hold values from -64 to 64
- query_weight: bfloat16 [8192, 4096], P(None, 'tp'), may hold values from -0.0625 to 0.0625
- keyval_weight: bfloat16 [8192, 2048], P(None, 'tp'), may hold values from -0.0625 to 0.0625
- doc_lengths: int32 [64], replicated, may hold values from 1 to 2048, 8192 in all
- owners: int32 [512], replicated, may hold values from 0 to 31, as said below
Outputs:
- attended: bfloat16 [8192, 4096], P('ctx', 'tp')
Inputs may be any that keep to these rules, and one draw needn't show every extreme that they name: The 16 blocks of one index of ctx (blocks i * 16 to (i + 1) * 16 - 1) go to 16 different owners; for each position j < 16, the blocks i * 16 + j of all indices i go to all different owners, so every owner receives exactly one block of each position.
All inputs are finite; a program needn't handle non-finite values.
Results may differ from a plain program's by a relative error of at most 0.0055.
The roundings to bfloat16 on the way count: a program that leaves them out, or rounds other values in their place, can miss the bound.
Values may be sent and summed in bfloat16 or wider, within the bound.
A program may use at most 128 MiB of HBM per device.

v0:
```python
import math
import jax
import jax.numpy as jnp
from jax import lax
from jax.sharding import PartitionSpec as P

NEG_FILL = -1e30


def token_places(block_order, first_row, row_count, block_len):
    row_index = first_row + jnp.arange(row_count, dtype=jnp.int32)
    return block_order[row_index // block_len] * block_len + row_index % block_len


def documents(token_place, doc_ends):
    return jnp.sum((doc_ends[None, :] <= token_place[:, None]).astype(jnp.int32), axis=1)


def body(tokens, query_weight, keyval_weight, doc_lengths, owners):
    cycle_count = lax.axis_size("ctx")
    device = lax.axis_index("ctx")
    group_count = lax.axis_size("tp")
    share_rows = tokens.shape[0]
    tok_rows = share_rows * group_count
    per_device = owners.shape[0] // cycle_count
    block_len = tok_rows // per_device
    head_dim = keyval_weight.shape[1] // 2
    query_cols = query_weight.shape[1]
    block_order = jnp.argsort(owners, stable=True)
    doc_ends = jnp.cumsum(doc_lengths)
    owner_grid = owners.reshape(cycle_count, per_device)
    own_targets = lax.dynamic_index_in_dim(owner_grid, device, 0, keepdims=False)
    piece = lax.all_gather(tokens, "tp", axis=0, tiled=True)
    query_part = jnp.dot(piece, query_weight, preferred_element_type=jnp.float32).astype(
        jnp.bfloat16
    )
    keyval_part = jnp.dot(piece, keyval_weight, preferred_element_type=jnp.float32).astype(
        jnp.bfloat16
    )
    projected = jnp.concatenate([query_part, keyval_part], axis=1)
    columns = projected.shape[1]
    blocks = projected.reshape(own_targets.shape[0], block_len, columns)
    arrived = lax.all_to_all(
        jnp.zeros((cycle_count, block_len, columns), projected.dtype).at[own_targets].set(blocks),
        "ctx",
        split_axis=0,
        concat_axis=0,
        tiled=True,
    )
    sources = jnp.nonzero(owners == device, size=per_device)[0] // per_device
    projected = arrived[sources].reshape(tok_rows, arrived.shape[2])
    queries = projected[:, :query_cols]
    keyvals = projected[:, query_cols:]
    heads_here = query_cols // head_dim
    score_scale = 1.0 / math.sqrt(head_dim)
    query_heads = queries.reshape(tok_rows, heads_here, head_dim).transpose(1, 0, 2)
    query_place = token_places(block_order, device * tok_rows, tok_rows, block_len)
    query_docs = documents(query_place, doc_ends)
    initial = (
        jnp.full((heads_here, tok_rows), NEG_FILL, jnp.float32),
        jnp.zeros((heads_here, tok_rows), jnp.float32),
        jnp.zeros((heads_here, tok_rows, head_dim), jnp.float32),
    )
    key_piece = lax.all_gather(keyvals, "ctx", axis=0, tiled=True)
    count_rows = key_piece.shape[0]
    sub_rows = math.gcd(count_rows, 512)
    key_place = token_places(block_order, jnp.int32(0), count_rows, block_len)
    key_docs = documents(key_place, doc_ends)
    stacked = (
        key_piece.reshape(count_rows // sub_rows, sub_rows, key_piece.shape[1]),
        key_place.reshape(count_rows // sub_rows, sub_rows),
        key_docs.reshape(count_rows // sub_rows, sub_rows),
    )

    def advance(partial_value, member):
        keyval, member_place, member_docs = member
        allowed = (member_docs[None, :] == query_docs[:, None]) & (
            member_place[None, :] <= query_place[:, None]
        )

        def update(current):
            run_max, run_sum, run_acc = current
            scores = (
                jnp.einsum(
                    "hqd,kd->hqk",
                    query_heads,
                    keyval[:, :head_dim],
                    preferred_element_type=jnp.float32,
                )
                * score_scale
            )
            scores = jnp.where(allowed[None], scores, NEG_FILL)
            new_max = jnp.maximum(run_max, jnp.max(scores, axis=2))
            weights = jnp.where(allowed[None], jnp.exp(scores - new_max[:, :, None]), 0.0)
            factor = jnp.exp(run_max - new_max)
            new_sum = run_sum * factor + jnp.sum(weights, axis=2)
            new_acc = run_acc * factor[:, :, None] + jnp.einsum(
                "hqk,kd->hqd",
                weights.astype(jnp.bfloat16),
                keyval[:, head_dim:],
                preferred_element_type=jnp.float32,
            )
            return (new_max, new_sum, new_acc)

        def unchanged(current):
            return current

        return (lax.cond(jnp.any(allowed), update, unchanged, partial_value), None)

    finished, unused = lax.scan(advance, initial, stacked)
    attended = finished[2] / finished[1][:, :, None]
    return attended.transpose(1, 0, 2).reshape(tok_rows, heads_here * head_dim).astype(jnp.bfloat16)


def solution(mesh):
    return jax.shard_map(
        body,
        mesh=mesh,
        in_specs=(P(("ctx", "tp"), None), P(None, "tp"), P(None, "tp"), P(), P()),
        out_specs=P("ctx", "tp"),
        check_vma=False,
    )
```

profile of v0, /device:TPU:1, one launch (start us, length us, event | category | flops | bytes accessed | tf_op | source)
XLA Modules:
  0.0 275.2 jit_solution(502739521675465678)
XLA Ops:
  8.2 59.6 %all-gather.3.cloned.1.call-done = bf16[256,8192]{1,0:T(8,128)(2,1)} async-done(((bf16[32,8192]{1,0:T(8,128)(2,1)}), bf16[256,8192]{1,0:T(8,128)(2,1)}) %all-gather.3.cloned.1.call-update) | async-done | bytes 4194320 | tf_op jit(solution)/shard_map/all_gather | solution.py:33
  67.8 7.1 %convolution_convert_fusion = bf16[256,512]{1,0:T(8,128)(2,1)S(1)} fusion(bf16[256,8192]{1,0:T(8,128)(2,1)} %all-gather.3.cloned.1.call-done, bf16[8192,512]{1,0:T(8,128)(2,1)} %param.10), kind=kOutput, calls=%fused_computation.28 | convolution fusion | flops 2147614720 | bytes 12845056 | tf_op jit(solution)/shard_map/dot_general | solution.py:34
  75.0 1.2 convolution_convert_fusion.1
  76.3 0.9 broadcast_in_dim.60
  77.2 2.5 scatter_fusion
  79.7 10.1 %all-to-all-start = ((bf16[32,16,768]{2,1,0:T(8,128)(2,1)}), bf16[32,16,768]{2,1,0:T(8,128)(2,1)S(1)}, u32[]{:S(2)}, u32[]{:S(2)}) async-start(bf16[32,16,768]{2,1,0:T(8,128)(2,1)} %scatter_fusion), calls=%async_computation | async-start | bytes 1572864 | tf_op jit(solution)/shard_map/all_to_all | solution.py:43
  91.2 4.1 %scatter_custom_fusion.1 = s32[16]{0:T(128)S(1)} fusion(s32[512]{0:T(512)S(1)} %bitcast.63, s32[512]{0:T(512)S(1)} %broadcast.398, s32[]{:T(128)} %copy.68), kind=kCustom, calls=%fused_computation.89 | custom fusion | flops 512 | bytes 68 | tf_op jit(solution)/shard_map/scatter-add | solution.py:50
  96.2 16.5 %all-to-all-done = bf16[32,16,768]{2,1,0:T(8,128)(2,1)S(1)} async-done(((bf16[32,16,768]{2,1,0:T(8,128)(2,1)}), bf16[32,16,768]{2,1,0:T(8,128)(2,1)S(1)}, u32[]{:S(2)}, u32[]{:S(2)}) %all-to-all-start) | async-done | bytes 786464 | tf_op jit(solution)/shard_map/all_to_all | solution.py:43
  114.3 3.8 %sort.17 = (s32[512]{0:T(512)}, s32[512]{0:T(512)S(1)}) sort(s32[512]{0:T(512)S(1)} %copy-done, s32[512]{0:T(512)S(1)} %iota.37), dimensions={0}, to_apply=%region_6.7 | sort | flops 4608 | bytes 8192 | tf_op jit(solution)/shard_map/jit(argsort)/sort | solution.py:29
  118.1 1.9 gather_fusion.1
  120.1 51.2 %gather_fusion = s32[8192]{0:T(1024)S(1)} fusion(s32[512]{0:T(512)S(1)} %get-tuple-element.106, s32[8192]{0:T(1024)S(1)} %broadcast_clamp_fusion), kind=kCustom, calls=%fused_computation | custom fusion | bytes 98304 | tf_op jit(solution)/shard_map/gather | solution.py:12
  172.2 23.5 %all-gather.5.cloned.1.call-done = bf16[8192,256]{1,0:T(8,128)(2,1)} async-done(((bf16[256,256]{1,0:T(8,128)(2,1)}), bf16[8192,256]{1,0:T(8,128)(2,1)}) %all-gather.5.cloned.1.call-update) | async-done | bytes 4194320 | tf_op jit(solution)/shard_map/all_gather | solution.py:64
  195.7 71.7 %while.14 = (s32[]{:T(128)}, f32[4,256]{1,0:T(4,128)S(1)}, f32[4,256]{1,0:T(4,128)S(1)}, f32[4,256,128]{2,1,0:T(8,128)S(1)}, s32[16,512]{1,0:T(8,128)S(1)}, /*in...) while((s32[]{:T(128)}, f32[4,256]{1,0:T(4,128)S(1)}, ...), condition=%wide.region_16.17_spmd, body=%wide.region_10.16_spmd.sunk | while | flops 276039680 | bytes 8993003 | solution.py:110
  195.8 0.8 fusion.37
  197.2 2.9 %conditional.2 = ((f32[4,256]{1,0:T(4,128)S(1)}, f32[4,256]{1,0:T(4,128)S(1)}, f32[4,256,128]{2,1,0:T(8,128)S(1)})) conditional(s32[]{:T(128)} %convert_element_type.54, (f32[4,256]{1,0:T(4,128)S(1)}, f32[4,256]{1,0:T(4,128)S(1)}, f32[4,256,128]{2,1,0:T(8,128)S(1)}) %tuple.42, (pred[256,512]{0,1:T(8,128)(4,1)S(1)}, ...), branch_computations={%region_12.12_spmd, %region_13.15_spmd} | conditional | flops 275515392 | bytes 8847396 | solution.py:108
  197.3 1.0 dynamic-slice_bitcast_fusion
  199.3 0.9 convolution_add_fusion
  200.2 0.8 fusion.37
  201.7 2.9 %conditional.2 = ((f32[4,256]{1,0:T(4,128)S(1)}, f32[4,256]{1,0:T(4,128)S(1)}, f32[4,256,128]{2,1,0:T(8,128)S(1)})) conditional(s32[]{:T(128)} %convert_element_type.54, (f32[4,256]{1,0:T(4,128)S(1)}, f32[4,256]{1,0:T(4,128)S(1)}, f32[4,256,128]{2,1,0:T(8,128)S(1)}) %tuple.42, (pred[256,512]{0,1:T(8,128)(4,1)S(1)}, ...), branch_computations={%region_12.12_spmd, %region_13.15_spmd} | conditional | flops 275515392 | bytes 8847396 | solution.py:108
  201.7 1.0 dynamic-slice_bitcast_fusion
  203.8 0.9 convolution_add_fusion
  206.2 2.9 %conditional.2 = ((f32[4,256]{1,0:T(4,128)S(1)}, f32[4,256]{1,0:T(4,128)S(1)}, f32[4,256,128]{2,1,0:T(8,128)S(1)})) conditional(s32[]{:T(128)} %convert_element_type.54, (f32[4,256]{1,0:T(4,128)S(1)}, f32[4,256]{1,0:T(4,128)S(1)}, f32[4,256,128]{2,1,0:T(8,128)S(1)}) %tuple.42, (pred[256,512]{0,1:T(8,128)(4,1)S(1)}, ...), branch_computations={%region_12.12_spmd, %region_13.15_spmd} | conditional | flops 275515392 | bytes 8847396 | solution.py:108
  206.2 1.0 dynamic-slice_bitcast_fusion
  208.3 0.9 convolution_add_fusion
  210.7 2.9 %conditional.2 = ((f32[4,256]{1,0:T(4,128)S(1)}, f32[4,256]{1,0:T(4,128)S(1)}, f32[4,256,128]{2,1,0:T(8,128)S(1)})) conditional(s32[]{:T(128)} %convert_element_type.54, (f32[4,256]{1,0:T(4,128)S(1)}, f32[4,256]{1,0:T(4,128)S(1)}, f32[4,256,128]{2,1,0:T(8,128)S(1)}) %tuple.42, (pred[256,512]{0,1:T(8,128)(4,1)S(1)}, ...), branch_computations={%region_12.12_spmd, %region_13.15_spmd} | conditional | flops 275515392 | bytes 8847396 | solution.py:108
  210.7 1.0 dynamic-slice_bitcast_fusion
  212.7 0.9 convolution_add_fusion
  215.2 2.9 %conditional.2 = ((f32[4,256]{1,0:T(4,128)S(1)}, f32[4,256]{1,0:T(4,128)S(1)}, f32[4,256,128]{2,1,0:T(8,128)S(1)})) conditional(s32[]{:T(128)} %convert_element_type.54, (f32[4,256]{1,0:T(4,128)S(1)}, f32[4,256]{1,0:T(4,128)S(1)}, f32[4,256,128]{2,1,0:T(8,128)S(1)}) %tuple.42, (pred[256,512]{0,1:T(8,128)(4,1)S(1)}, ...), branch_computations={%region_12.12_spmd, %region_13.15_spmd} | conditional | flops 275515392 | bytes 8847396 | solution.py:108
  215.2 1.0 dynamic-slice_bitcast_fusion
  217.2 0.9 convolution_add_fusion
  219.6 2.9 %conditional.2 = ((f32[4,256]{1,0:T(4,128)S(1)}, f32[4,256]{1,0:T(4,128)S(1)}, f32[4,256,128]{2,1,0:T(8,128)S(1)})) conditional(s32[]{:T(128)} %convert_element_type.54, (f32[4,256]{1,0:T(4,128)S(1)}, f32[4,256]{1,0:T(4,128)S(1)}, f32[4,256,128]{2,1,0:T(8,128)S(1)}) %tuple.42, (pred[256,512]{0,1:T(8,128)(4,1)S(1)}, ...), branch_computations={%region_12.12_spmd, %region_13.15_spmd} | conditional | flops 275515392 | bytes 8847396 | solution.py:108
  219.7 1.0 dynamic-slice_bitcast_fusion
  221.7 0.9 convolution_add_fusion
  224.1 2.9 %conditional.2 = ((f32[4,256]{1,0:T(4,128)S(1)}, f32[4,256]{1,0:T(4,128)S(1)}, f32[4,256,128]{2,1,0:T(8,128)S(1)})) conditional(s32[]{:T(128)} %convert_element_type.54, (f32[4,256]{1,0:T(4,128)S(1)}, f32[4,256]{1,0:T(4,128)S(1)}, f32[4,256,128]{2,1,0:T(8,128)S(1)}) %tuple.42, (pred[256,512]{0,1:T(8,128)(4,1)S(1)}, ...), branch_computations={%region_12.12_spmd, %region_13.15_spmd} | conditional | flops 275515392 | bytes 8847396 | solution.py:108
  224.1 1.0 dynamic-slice_bitcast_fusion
  226.2 0.9 convolution_add_fusion
  228.6 2.9 %conditional.2 = ((f32[4,256]{1,0:T(4,128)S(1)}, f32[4,256]{1,0:T(4,128)S(1)}, f32[4,256,128]{2,1,0:T(8,128)S(1)})) conditional(s32[]{:T(128)} %convert_element_type.54, (f32[4,256]{1,0:T(4,128)S(1)}, f32[4,256]{1,0:T(4,128)S(1)}, f32[4,256,128]{2,1,0:T(8,128)S(1)}) %tuple.42, (pred[256,512]{0,1:T(8,128)(4,1)S(1)}, ...), branch_computations={%region_12.12_spmd, %region_13.15_spmd} | conditional | flops 275515392 | bytes 8847396 | solution.py:108
  228.6 1.0 dynamic-slice_bitcast_fusion
  230.7 0.9 convolution_add_fusion
  233.1 2.9 %conditional.2 = ((f32[4,256]{1,0:T(4,128)S(1)}, f32[4,256]{1,0:T(4,128)S(1)}, f32[4,256,128]{2,1,0:T(8,128)S(1)})) conditional(s32[]{:T(128)} %convert_element_type.54, (f32[4,256]{1,0:T(4,128)S(1)}, f32[4,256]{1,0:T(4,128)S(1)}, f32[4,256,128]{2,1,0:T(8,128)S(1)}) %tuple.42, (pred[256,512]{0,1:T(8,128)(4,1)S(1)}, ...), branch_computations={%region_12.12_spmd, %region_13.15_spmd} | conditional | flops 275515392 | bytes 8847396 | solution.py:108
  233.1 1.0 dynamic-slice_bitcast_fusion
  235.1 0.9 convolution_add_fusion
  237.6 2.9 %conditional.2 = ((f32[4,256]{1,0:T(4,128)S(1)}, f32[4,256]{1,0:T(4,128)S(1)}, f32[4,256,128]{2,1,0:T(8,128)S(1)})) conditional(s32[]{:T(128)} %convert_element_type.54, (f32[4,256]{1,0:T(4,128)S(1)}, f32[4,256]{1,0:T(4,128)S(1)}, f32[4,256,128]{2,1,0:T(8,128)S(1)}) %tuple.42, (pred[256,512]{0,1:T(8,128)(4,1)S(1)}, ...), branch_computations={%region_12.12_spmd, %region_13.15_spmd} | conditional | flops 275515392 | bytes 8847396 | solution.py:108
  237.6 1.0 dynamic-slice_bitcast_fusion
  239.6 0.9 convolution_add_fusion
  242.0 2.9 %conditional.2 = ((f32[4,256]{1,0:T(4,128)S(1)}, f32[4,256]{1,0:T(4,128)S(1)}, f32[4,256,128]{2,1,0:T(8,128)S(1)})) conditional(s32[]{:T(128)} %convert_element_type.54, (f32[4,256]{1,0:T(4,128)S(1)}, f32[4,256]{1,0:T(4,128)S(1)}, f32[4,256,128]{2,1,0:T(8,128)S(1)}) %tuple.42, (pred[256,512]{0,1:T(8,128)(4,1)S(1)}, ...), branch_computations={%region_12.12_spmd, %region_13.15_spmd} | conditional | flops 275515392 | bytes 8847396 | solution.py:108
  242.1 1.0 dynamic-slice_bitcast_fusion
  244.1 0.9 convolution_add_fusion
  246.5 2.9 %conditional.2 = ((f32[4,256]{1,0:T(4,128)S(1)}, f32[4,256]{1,0:T(4,128)S(1)}, f32[4,256,128]{2,1,0:T(8,128)S(1)})) conditional(s32[]{:T(128)} %convert_element_type.54, (f32[4,256]{1,0:T(4,128)S(1)}, f32[4,256]{1,0:T(4,128)S(1)}, f32[4,256,128]{2,1,0:T(8,128)S(1)}) %tuple.42, (pred[256,512]{0,1:T(8,128)(4,1)S(1)}, ...), branch_computations={%region_12.12_spmd, %region_13.15_spmd} | conditional | flops 275515392 | bytes 8847396 | solution.py:108
  246.5 1.0 dynamic-slice_bitcast_fusion
  248.6 0.9 convolution_add_fusion
  251.0 2.9 %conditional.2 = ((f32[4,256]{1,0:T(4,128)S(1)}, f32[4,256]{1,0:T(4,128)S(1)}, f32[4,256,128]{2,1,0:T(8,128)S(1)})) conditional(s32[]{:T(128)} %convert_element_type.54, (f32[4,256]{1,0:T(4,128)S(1)}, f32[4,256]{1,0:T(4,128)S(1)}, f32[4,256,128]{2,1,0:T(8,128)S(1)}) %tuple.42, (pred[256,512]{0,1:T(8,128)(4,1)S(1)}, ...), branch_computations={%region_12.12_spmd, %region_13.15_spmd} | conditional | flops 275515392 | bytes 8847396 | solution.py:108
  251.0 1.0 dynamic-slice_bitcast_fusion
  253.1 0.9 convolution_add_fusion
  255.5 2.9 %conditional.2 = ((f32[4,256]{1,0:T(4,128)S(1)}, f32[4,256]{1,0:T(4,128)S(1)}, f32[4,256,128]{2,1,0:T(8,128)S(1)})) conditional(s32[]{:T(128)} %convert_element_type.54, (f32[4,256]{1,0:T(4,128)S(1)}, f32[4,256]{1,0:T(4,128)S(1)}, f32[4,256,128]{2,1,0:T(8,128)S(1)}) %tuple.42, (pred[256,512]{0,1:T(8,128)(4,1)S(1)}, ...), branch_computations={%region_12.12_spmd, %region_13.15_spmd} | conditional | flops 275515392 | bytes 8847396 | solution.py:108
  255.5 1.0 dynamic-slice_bitcast_fusion
  257.5 0.9 convolution_add_fusion
  260.0 2.9 %conditional.2 = ((f32[4,256]{1,0:T(4,128)S(1)}, f32[4,256]{1,0:T(4,128)S(1)}, f32[4,256,128]{2,1,0:T(8,128)S(1)})) conditional(s32[]{:T(128)} %convert_element_type.54, (f32[4,256]{1,0:T(4,128)S(1)}, f32[4,256]{1,0:T(4,128)S(1)}, f32[4,256,128]{2,1,0:T(8,128)S(1)}) %tuple.42, (pred[256,512]{0,1:T(8,128)(4,1)S(1)}, ...), branch_computations={%region_12.12_spmd, %region_13.15_spmd} | conditional | flops 275515392 | bytes 8847396 | solution.py:108
  260.0 1.0 dynamic-slice_bitcast_fusion
  262.0 0.9 convolution_add_fusion
  264.4 2.9 %conditional.2 = ((f32[4,256]{1,0:T(4,128)S(1)}, f32[4,256]{1,0:T(4,128)S(1)}, f32[4,256,128]{2,1,0:T(8,128)S(1)})) conditional(s32[]{:T(128)} %convert_element_type.54, (f32[4,256]{1,0:T(4,128)S(1)}, f32[4,256]{1,0:T(4,128)S(1)}, f32[4,256,128]{2,1,0:T(8,128)S(1)}) %tuple.42, (pred[256,512]{0,1:T(8,128)(4,1)S(1)}, ...), branch_computations={%region_12.12_spmd, %region_13.15_spmd} | conditional | flops 275515392 | bytes 8847396 | solution.py:108
  264.5 1.0 dynamic-slice_bitcast_fusion
  266.5 0.9 convolution_add_fusion
  267.4 0.9 copy_bitcast_fusion
  (163 shorter events, 35.2 us)
Async XLA Ops:
  6.5 61.3 %all-gather.3.cloned.1.call-start = ((), (), s32[]{:S(2)}) async-start(), calls=%async_computation.1 | async-start | bytes 4718592 | tf_op jit(solution)/shard_map/all_gather | solution.py:33
  67.8 7.1 %copy-start.2 = (bf16[8192,256]{1,0:T(8,128)(2,1)S(1)}, bf16[8192,256]{1,0:T(8,128)(2,1)}, u32[]{:S(2)}) copy-start(bf16[8192,256]{1,0:T(8,128)(2,1)} %param.11) | copy-start | bytes 12582916
  67.8 7.1 %copy-start.3 = (bf16[256,8192]{1,0:T(8,128)(2,1)S(1)}, bf16[256,8192]{1,0:T(8,128)(2,1)}, u32[]{:S(2)}) copy-start(bf16[256,8192]{1,0:T(8,128)(2,1)} %all-gather.3.cloned.1.call-done) | copy-start | bytes 12582916
  76.2 13.7 %copy-start = (s32[512]{0:T(512)S(1)}, s32[512]{0:T(512)}, u32[]{:S(2)}) copy-start(s32[512]{0:T(512)} %param.13) | copy-start | bytes 6148
  77.2 36.7 %copy-start.1 = (s32[64]{0:T(128)S(1)}, s32[64]{0:T(128)}, u32[]{:S(2)}) copy-start(s32[64]{0:T(128)} %param.12) | copy-start | bytes 772
  79.7 32.9 %all-to-all-start = ((bf16[32,16,768]{2,1,0:T(8,128)(2,1)}), bf16[32,16,768]{2,1,0:T(8,128)(2,1)S(1)}, u32[]{:S(2)}, u32[]{:S(2)}) async-start(bf16[32,16,768]{2,1,0:T(8,128)(2,1)} %scatter_fusion), calls=%async_computation | async-start | bytes 1572864 | tf_op jit(solution)/shard_map/all_to_all | solution.py:43
  89.9 105.8 %all-gather.5.cloned.1.call-start = ((), (), s32[]{:S(2)}) async-start(), calls=%async_computation.2 | async-start | bytes 4325376 | tf_op jit(solution)/shard_map/all_gather | solution.py:64
Sparse Core Ops, SparseCore 0:
  9.1 58.6 all-gather.2
  114.1 81.5 all-gather.4
where the time goes:
time: 276 us; the launch traced here: 275 us
  waiting for transfers between devices  100 us (36%)
  local copies, waits for them, and re-layouts  75.3 us (27%)
  other arithmetic  33.8 us (12%)
  matrix products  30.3 us (11%)
  between operations  13.6 us (5%)
  loops' own time  11.6 us (4%)
  starting transfers between devices  10.2 us (4%)
    all_gather x1, waiting for transfers between devices, body(): piece = lax.all_gather(tokens, 'tp', axis=0, tiled=True)  59.6 us
    gather x2, local copies, waits for them, and re-layouts, token_places(): block_order[row_index // block_len] * block_len + row_index % block_len  53.2 us
    all_gather x1, waiting for transfers between devices, body(): key_piece = lax.all_gather(keyvals, 'ctx', axis=0, tiled=True)  23.5 us
    all_to_all x1, waiting for transfers between devices, body(): lax.all_to_all(jnp.zeros((cycle_count, block_len, columns), projected.dty...  16.5 us
    squeeze x16, local copies, waits for them, and re-layouts, body(): finished, unused = lax.scan(advance, initial, stacked)  15.6 us
    dot_general x16, matrix products, update(): jnp.einsum('hqk,kd->hqd', weights.astype(jnp.bfloat16), keyval[:, head_di...  13.9 us
    reduce_or x16, other arithmetic, advance(): return (lax.cond(jnp.any(allowed), update, unchanged, partial_value), None)  13.4 us
    another operation x1, loops' own time, body(): finished, unused = lax.scan(advance, initial, stacked)  10.9 us
  transfers between devices with their start and end apart: 3, of which 3 were waited for; matrix products, arithmetic and copies ran while one was open for 24% of the time, Pallas kernels for 0%

commit v1 on v0

--- a/solution.py
+++ b/solution.py
@@ -30,7 +30,9 @@
     doc_ends = jnp.cumsum(doc_lengths)
     owner_grid = owners.reshape(cycle_count, per_device)
     own_targets = lax.dynamic_index_in_dim(owner_grid, device, 0, keepdims=False)
-    piece = lax.all_gather(tokens, "tp", axis=0, tiled=True)
+    piece = jnp.concatenate(
+        lax.all_to_all(jnp.stack([tokens] * lax.axis_size("tp")), "tp", 0, 0), axis=0
+    )
     query_part = jnp.dot(piece, query_weight, preferred_element_type=jnp.float32).astype(
         jnp.bfloat16
     )

time: 276 us -> 292 us (1.058)
  starting transfers between devices: 10.2 us -> 17.7 us
  waiting for transfers between devices: 100 us -> 104 us
    all_gather x1 -> x0, waiting for transfers between devices: 59.6 us -> none  [body(): piece = lax.all_gather(tokens, 'tp', axis=0, tiled=True)]
    all_to_all x0 -> x1, waiting for transfers between devices: none -> 49.4 us  [body(): lax.all_to_all(jnp.stack([tokens] * lax.axis_size('tp')), 'tp', 0, 0)]
    all_gather x1, waiting for transfers between devices: 23.5 us -> 37.8 us  [body(): key_piece = lax.all_gather(keyvals, 'ctx', axis=0, tiled=True)]
    all_to_all x0 -> x1, starting transfers between devices: none -> 5.98 us  [body(): lax.all_to_all(jnp.stack([tokens] * lax.axis_size('tp')), 'tp', 0, 0)]
    another operation x3 -> x4, local copies, waits for them, and re-layouts: 0.3 us -> 3.8 us  [the longest x1 3.5 us: body(): jnp.stack([tokens] * lax.axis_size('tp'))]
  transfers between devices with their start and end apart: 3 -> 3, of which waited for: 3 -> 3; matrix products, arithmetic and copies ran while one was open for 24% -> 22% of each run, Pallas kernels for 0% -> 0%
where the time goes in v1:
time: 292 us; the launch traced here: 291 us
  waiting for transfers between devices  104 us (36%)
  local copies, waits for them, and re-layouts  78.1 us (27%)
  other arithmetic  33.8 us (12%)
  matrix products  32.5 us (11%)
  starting transfers between devices  17.7 us (6%)
  between operations  13.6 us (5%)
  loops' own time  11.6 us (4%)
    gather x2, local copies, waits for them, and re-layouts, token_places(): block_order[row_index // block_len] * block_len + row_index % block_len  53.2 us
    all_to_all x1, waiting for transfers between devices, body(): lax.all_to_all(jnp.stack([tokens] * lax.axis_size('tp')), 'tp', 0, 0)  49.4 us
    all_gather x1, waiting for transfers between devices, body(): key_piece = lax.all_gather(keyvals, 'ctx', axis=0, tiled=True)  37.8 us
    all_to_all x1, waiting for transfers between devices, body(): lax.all_to_all(jnp.zeros((cycle_count, block_len, columns), projected.dty...  16.5 us
    squeeze x16, local copies, waits for them, and re-layouts, body(): finished, unused = lax.scan(advance, initial, stacked)  15.6 us
    dot_general x16, matrix products, update(): jnp.einsum('hqk,kd->hqd', weights.astype(jnp.bfloat16), keyval[:, head_di...  13.9 us
    reduce_or x16, other arithmetic, advance(): return (lax.cond(jnp.any(allowed), update, unchanged, partial_value), None)  13.4 us
    all_to_all x1, starting transfers between devices, body(): lax.all_to_all(jnp.zeros((cycle_count, block_len, columns), projected.dty...  11.7 us
  transfers between devices with their start and end apart: 3, of which 3 were waited for; matrix products, arithmetic and copies ran while one was open for 22% of the time, Pallas kernels for 0%

profile of v1, /device:TPU:1, one launch (start us, length us, event | category | flops | bytes accessed | tf_op | source)
XLA Modules:
  0.0 291.0 jit_solution(3404569222870240396)
XLA Ops:
  6.5 3.5 %stack.2 = bf16[8,32,8192]{2,1,0:T(8,128)(2,1)} broadcast(bf16[32,8192]{1,0:T(8,128)(2,1)} %param.9), dimensions={1,2} | broadcast | bytes 4718592 | tf_op jit(solution)/shard_map/stack | solution.py:34
  10.0 6.0 %all-to-all-start = ((bf16[8,32,8192]{2,1,0:T(8,128)(2,1)}), bf16[8,32,8192]{2,1,0:T(8,128)(2,1)}, u32[]{:S(2)}, u32[]{:S(2)}) async-start(bf16[8,32,8192]{2,1,0:T(8,128)(2,1)} %stack.2), calls=%async_computation | async-start | bytes 8388608 | tf_op jit(solution)/shard_map/all_to_all | solution.py:34
  16.3 49.4 %all-to-all-done = bf16[8,32,8192]{2,1,0:T(8,128)(2,1)} async-done(((bf16[8,32,8192]{2,1,0:T(8,128)(2,1)}), bf16[8,32,8192]{2,1,0:T(8,128)(2,1)}, u32[]{:S(2)}, u32[]{:S(2)}) %all-to-all-start) | async-done | bytes 4194336 | tf_op jit(solution)/shard_map/all_to_all | solution.py:34
  65.7 7.1 %convolution_convert_fusion = bf16[256,512]{1,0:T(8,128)(2,1)S(1)} fusion(bf16[256,8192]{1,0:T(8,128)(2,1)} %bitcast.10, bf16[8192,512]{1,0:T(8,128)(2,1)} %param.10), kind=kOutput, calls=%fused_computation.28 | convolution fusion | flops 2147614720 | bytes 12845056 | tf_op jit(solution)/shard_map/dot_general | solution.py:36
  72.8 3.4 %convolution_convert_fusion.1 = bf16[256,256]{1,0:T(8,128)(2,1)S(1)} fusion(bf16[256,8192]{1,0:T(8,128)(2,1)} %bitcast.10, bf16[8192,256]{1,0:T(8,128)(2,1)S(1)} %copy-done.2), kind=kOutput, calls=%fused_computation.29 | convolution fusion | flops 1073807360 | bytes 8519680 | tf_op jit(solution)/shard_map/dot_general | solution.py:39
  76.3 0.9 broadcast_in_dim.60
  77.2 2.5 scatter_fusion
  79.8 11.7 %all-to-all-start.1 = ((bf16[32,16,768]{2,1,0:T(8,128)(2,1)}), bf16[32,16,768]{2,1,0:T(8,128)(2,1)S(1)}, u32[]{:S(2)}, u32[]{:S(2)}) async-start(bf16[32,16,768]{2,1,0:T(8,128)(2,1)} %scatter_fusion), calls=%async_computation.1 | async-start | bytes 1572864 | tf_op jit(solution)/shard_map/all_to_all | solution.py:45
  92.8 4.1 %scatter_custom_fusion.1 = s32[16]{0:T(128)S(1)} fusion(s32[512]{0:T(512)S(1)} %bitcast.64, s32[512]{0:T(512)S(1)} %broadcast.400, s32[]{:T(128)} %copy.68), kind=kCustom, calls=%fused_computation.89 | custom fusion | flops 512 | bytes 68 | tf_op jit(solution)/shard_map/scatter-add | solution.py:52
  97.8 16.5 %all-to-all-done.1 = bf16[32,16,768]{2,1,0:T(8,128)(2,1)S(1)} async-done(((bf16[32,16,768]{2,1,0:T(8,128)(2,1)}), bf16[32,16,768]{2,1,0:T(8,128)(2,1)S(1)}, u32[]{:S(2)}, u32[]{:S(2)}) %all-to-all-start.1) | async-done | bytes 786464 | tf_op jit(solution)/shard_map/all_to_all | solution.py:45
  115.9 3.8 %sort.17 = (s32[512]{0:T(512)}, s32[512]{0:T(512)S(1)}) sort(s32[512]{0:T(512)S(1)} %copy-done, s32[512]{0:T(512)S(1)} %iota.37), dimensions={0}, to_apply=%region_6.7 | sort | flops 4608 | bytes 8192 | tf_op jit(solution)/shard_map/jit(argsort)/sort | solution.py:29
  119.7 1.9 gather_fusion.1
  121.7 51.2 %gather_fusion = s32[8192]{0:T(1024)S(1)} fusion(s32[512]{0:T(512)S(1)} %get-tuple-element.106, s32[8192]{0:T(1024)S(1)} %broadcast_clamp_fusion), kind=kCustom, calls=%fused_computation | custom fusion | bytes 98304 | tf_op jit(solution)/shard_map/gather | solution.py:12
  173.8 37.8 %all-gather.2.cloned.1.call-done = bf16[8192,256]{1,0:T(8,128)(2,1)} async-done(((bf16[256,256]{1,0:T(8,128)(2,1)}), bf16[8192,256]{1,0:T(8,128)(2,1)}) %all-gather.2.cloned.1.call-update) | async-done | bytes 4194320 | tf_op jit(solution)/shard_map/all_gather | solution.py:66
  211.6 71.7 %while.14 = (s32[]{:T(128)}, f32[4,256]{1,0:T(4,128)S(1)}, f32[4,256]{1,0:T(4,128)S(1)}, f32[4,256,128]{2,1,0:T(8,128)S(1)}, s32[16,512]{1,0:T(8,128)S(1)}, /*in...) while((s32[]{:T(128)}, f32[4,256]{1,0:T(4,128)S(1)}, ...), condition=%wide.region_16.17_spmd, body=%wide.region_10.16_spmd.sunk | while | flops 276039680 | bytes 8993003 | solution.py:112
  213.1 2.9 %conditional.2 = ((f32[4,256]{1,0:T(4,128)S(1)}, f32[4,256]{1,0:T(4,128)S(1)}, f32[4,256,128]{2,1,0:T(8,128)S(1)})) conditional(s32[]{:T(128)} %convert_element_type.54, (f32[4,256]{1,0:T(4,128)S(1)}, f32[4,256]{1,0:T(4,128)S(1)}, f32[4,256,128]{2,1,0:T(8,128)S(1)}) %tuple.42, (pred[256,512]{0,1:T(8,128)(4,1)S(1)}, ...), branch_computations={%region_12.12_spmd, %region_13.15_spmd} | conditional | flops 275515392 | bytes 8847396 | solution.py:110
  213.1 1.0 dynamic-slice_bitcast_fusion
  215.2 0.9 convolution_add_fusion
  217.6 2.9 %conditional.2 = ((f32[4,256]{1,0:T(4,128)S(1)}, f32[4,256]{1,0:T(4,128)S(1)}, f32[4,256,128]{2,1,0:T(8,128)S(1)})) conditional(s32[]{:T(128)} %convert_element_type.54, (f32[4,256]{1,0:T(4,128)S(1)}, f32[4,256]{1,0:T(4,128)S(1)}, f32[4,256,128]{2,1,0:T(8,128)S(1)}) %tuple.42, (pred[256,512]{0,1:T(8,128)(4,1)S(1)}, ...), branch_computations={%region_12.12_spmd, %region_13.15_spmd} | conditional | flops 275515392 | bytes 8847396 | solution.py:110
  217.6 1.0 dynamic-slice_bitcast_fusion
  219.7 0.9 convolution_add_fusion
  222.1 2.9 %conditional.2 = ((f32[4,256]{1,0:T(4,128)S(1)}, f32[4,256]{1,0:T(4,128)S(1)}, f32[4,256,128]{2,1,0:T(8,128)S(1)})) conditional(s32[]{:T(128)} %convert_element_type.54, (f32[4,256]{1,0:T(4,128)S(1)}, f32[4,256]{1,0:T(4,128)S(1)}, f32[4,256,128]{2,1,0:T(8,128)S(1)}) %tuple.42, (pred[256,512]{0,1:T(8,128)(4,1)S(1)}, ...), branch_computations={%region_12.12_spmd, %region_13.15_spmd} | conditional | flops 275515392 | bytes 8847396 | solution.py:110
  222.1 1.0 dynamic-slice_bitcast_fusion
  224.1 0.9 convolution_add_fusion
  226.6 2.9 %conditional.2 = ((f32[4,256]{1,0:T(4,128)S(1)}, f32[4,256]{1,0:T(4,128)S(1)}, f32[4,256,128]{2,1,0:T(8,128)S(1)})) conditional(s32[]{:T(128)} %convert_element_type.54, (f32[4,256]{1,0:T(4,128)S(1)}, f32[4,256]{1,0:T(4,128)S(1)}, f32[4,256,128]{2,1,0:T(8,128)S(1)}) %tuple.42, (pred[256,512]{0,1:T(8,128)(4,1)S(1)}, ...), branch_computations={%region_12.12_spmd, %region_13.15_spmd} | conditional | flops 275515392 | bytes 8847396 | solution.py:110
  226.6 1.0 dynamic-slice_bitcast_fusion
  228.6 0.9 convolution_add_fusion
  231.0 2.9 %conditional.2 = ((f32[4,256]{1,0:T(4,128)S(1)}, f32[4,256]{1,0:T(4,128)S(1)}, f32[4,256,128]{2,1,0:T(8,128)S(1)})) conditional(s32[]{:T(128)} %convert_element_type.54, (f32[4,256]{1,0:T(4,128)S(1)}, f32[4,256]{1,0:T(4,128)S(1)}, f32[4,256,128]{2,1,0:T(8,128)S(1)}) %tuple.42, (pred[256,512]{0,1:T(8,128)(4,1)S(1)}, ...), branch_computations={%region_12.12_spmd, %region_13.15_spmd} | conditional | flops 275515392 | bytes 8847396 | solution.py:110
  231.1 1.0 dynamic-slice_bitcast_fusion
  233.1 0.9 convolution_add_fusion
  235.5 2.9 %conditional.2 = ((f32[4,256]{1,0:T(4,128)S(1)}, f32[4,256]{1,0:T(4,128)S(1)}, f32[4,256,128]{2,1,0:T(8,128)S(1)})) conditional(s32[]{:T(128)} %convert_element_type.54, (f32[4,256]{1,0:T(4,128)S(1)}, f32[4,256]{1,0:T(4,128)S(1)}, f32[4,256,128]{2,1,0:T(8,128)S(1)}) %tuple.42, (pred[256,512]{0,1:T(8,128)(4,1)S(1)}, ...), branch_computations={%region_12.12_spmd, %region_13.15_spmd} | conditional | flops 275515392 | bytes 8847396 | solution.py:110
  235.5 1.0 dynamic-slice_bitcast_fusion
  237.6 0.9 convolution_add_fusion
  240.0 2.9 %conditional.2 = ((f32[4,256]{1,0:T(4,128)S(1)}, f32[4,256]{1,0:T(4,128)S(1)}, f32[4,256,128]{2,1,0:T(8,128)S(1)})) conditional(s32[]{:T(128)} %convert_element_type.54, (f32[4,256]{1,0:T(4,128)S(1)}, f32[4,256]{1,0:T(4,128)S(1)}, f32[4,256,128]{2,1,0:T(8,128)S(1)}) %tuple.42, (pred[256,512]{0,1:T(8,128)(4,1)S(1)}, ...), branch_computations={%region_12.12_spmd, %region_13.15_spmd} | conditional | flops 275515392 | bytes 8847396 | solution.py:110
  240.0 1.0 dynamic-slice_bitcast_fusion
  242.1 0.9 convolution_add_fusion
  244.5 2.9 %conditional.2 = ((f32[4,256]{1,0:T(4,128)S(1)}, f32[4,256]{1,0:T(4,128)S(1)}, f32[4,256,128]{2,1,0:T(8,128)S(1)})) conditional(s32[]{:T(128)} %convert_element_type.54, (f32[4,256]{1,0:T(4,128)S(1)}, f32[4,256]{1,0:T(4,128)S(1)}, f32[4,256,128]{2,1,0:T(8,128)S(1)}) %tuple.42, (pred[256,512]{0,1:T(8,128)(4,1)S(1)}, ...), branch_computations={%region_12.12_spmd, %region_13.15_spmd} | conditional | flops 275515392 | bytes 8847396 | solution.py:110
  244.5 1.0 dynamic-slice_bitcast_fusion
  246.5 0.9 convolution_add_fusion
  249.0 2.9 %conditional.2 = ((f32[4,256]{1,0:T(4,128)S(1)}, f32[4,256]{1,0:T(4,128)S(1)}, f32[4,256,128]{2,1,0:T(8,128)S(1)})) conditional(s32[]{:T(128)} %convert_element_type.54, (f32[4,256]{1,0:T(4,128)S(1)}, f32[4,256]{1,0:T(4,128)S(1)}, f32[4,256,128]{2,1,0:T(8,128)S(1)}) %tuple.42, (pred[256,512]{0,1:T(8,128)(4,1)S(1)}, ...), branch_computations={%region_12.12_spmd, %region_13.15_spmd} | conditional | flops 275515392 | bytes 8847396 | solution.py:110
  249.0 1.0 dynamic-slice_bitcast_fusion
  251.0 0.9 convolution_add_fusion
  253.4 2.9 %conditional.2 = ((f32[4,256]{1,0:T(4,128)S(1)}, f32[4,256]{1,0:T(4,128)S(1)}, f32[4,256,128]{2,1,0:T(8,128)S(1)})) conditional(s32[]{:T(128)} %convert_element_type.54, (f32[4,256]{1,0:T(4,128)S(1)}, f32[4,256]{1,0:T(4,128)S(1)}, f32[4,256,128]{2,1,0:T(8,128)S(1)}) %tuple.42, (pred[256,512]{0,1:T(8,128)(4,1)S(1)}, ...), branch_computations={%region_12.12_spmd, %region_13.15_spmd} | conditional | flops 275515392 | bytes 8847396 | solution.py:110
  253.5 1.0 dynamic-slice_bitcast_fusion
  255.5 0.9 convolution_add_fusion
  257.9 2.9 %conditional.2 = ((f32[4,256]{1,0:T(4,128)S(1)}, f32[4,256]{1,0:T(4,128)S(1)}, f32[4,256,128]{2,1,0:T(8,128)S(1)})) conditional(s32[]{:T(128)} %convert_element_type.54, (f32[4,256]{1,0:T(4,128)S(1)}, f32[4,256]{1,0:T(4,128)S(1)}, f32[4,256,128]{2,1,0:T(8,128)S(1)}) %tuple.42, (pred[256,512]{0,1:T(8,128)(4,1)S(1)}, ...), branch_computations={%region_12.12_spmd, %region_13.15_spmd} | conditional | flops 275515392 | bytes 8847396 | solution.py:110
  257.9 1.0 dynamic-slice_bitcast_fusion
  260.0 0.9 convolution_add_fusion
  262.4 2.9 %conditional.2 = ((f32[4,256]{1,0:T(4,128)S(1)}, f32[4,256]{1,0:T(4,128)S(1)}, f32[4,256,128]{2,1,0:T(8,128)S(1)})) conditional(s32[]{:T(128)} %convert_element_type.54, (f32[4,256]{1,0:T(4,128)S(1)}, f32[4,256]{1,0:T(4,128)S(1)}, f32[4,256,128]{2,1,0:T(8,128)S(1)}) %tuple.42, (pred[256,512]{0,1:T(8,128)(4,1)S(1)}, ...), branch_computations={%region_12.12_spmd, %region_13.15_spmd} | conditional | flops 275515392 | bytes 8847396 | solution.py:110
  262.4 1.0 dynamic-slice_bitcast_fusion
  264.5 0.9 convolution_add_fusion
  266.9 2.9 %conditional.2 = ((f32[4,256]{1,0:T(4,128)S(1)}, f32[4,256]{1,0:T(4,128)S(1)}, f32[4,256,128]{2,1,0:T(8,128)S(1)})) conditional(s32[]{:T(128)} %convert_element_type.54, (f32[4,256]{1,0:T(4,128)S(1)}, f32[4,256]{1,0:T(4,128)S(1)}, f32[4,256,128]{2,1,0:T(8,128)S(1)}) %tuple.42, (pred[256,512]{0,1:T(8,128)(4,1)S(1)}, ...), branch_computations={%region_12.12_spmd, %region_13.15_spmd} | conditional | flops 275515392 | bytes 8847396 | solution.py:110
  266.9 1.0 dynamic-slice_bitcast_fusion
  268.9 0.9 convolution_add_fusion
  271.4 2.9 %conditional.2 = ((f32[4,256]{1,0:T(4,128)S(1)}, f32[4,256]{1,0:T(4,128)S(1)}, f32[4,256,128]{2,1,0:T(8,128)S(1)})) conditional(s32[]{:T(128)} %convert_element_type.54, (f32[4,256]{1,0:T(4,128)S(1)}, f32[4,256]{1,0:T(4,128)S(1)}, f32[4,256,128]{2,1,0:T(8,128)S(1)}) %tuple.42, (pred[256,512]{0,1:T(8,128)(4,1)S(1)}, ...), branch_computations={%region_12.12_spmd, %region_13.15_spmd} | conditional | flops 275515392 | bytes 8847396 | solution.py:110
  271.4 1.0 dynamic-slice_bitcast_fusion
  273.4 0.9 convolution_add_fusion
  275.8 2.9 %conditional.2 = ((f32[4,256]{1,0:T(4,128)S(1)}, f32[4,256]{1,0:T(4,128)S(1)}, f32[4,256,128]{2,1,0:T(8,128)S(1)})) conditional(s32[]{:T(128)} %convert_element_type.54, (f32[4,256]{1,0:T(4,128)S(1)}, f32[4,256]{1,0:T(4,128)S(1)}, f32[4,256,128]{2,1,0:T(8,128)S(1)}) %tuple.42, (pred[256,512]{0,1:T(8,128)(4,1)S(1)}, ...), branch_computations={%region_12.12_spmd, %region_13.15_spmd} | conditional | flops 275515392 | bytes 8847396 | solution.py:110
  275.9 1.0 dynamic-slice_bitcast_fusion
  277.9 0.9 convolution_add_fusion
  280.3 2.9 %conditional.2 = ((f32[4,256]{1,0:T(4,128)S(1)}, f32[4,256]{1,0:T(4,128)S(1)}, f32[4,256,128]{2,1,0:T(8,128)S(1)})) conditional(s32[]{:T(128)} %convert_element_type.54, (f32[4,256]{1,0:T(4,128)S(1)}, f32[4,256]{1,0:T(4,128)S(1)}, f32[4,256,128]{2,1,0:T(8,128)S(1)}) %tuple.42, (pred[256,512]{0,1:T(8,128)(4,1)S(1)}, ...), branch_computations={%region_12.12_spmd, %region_13.15_spmd} | conditional | flops 275515392 | bytes 8847396 | solution.py:110
  280.3 1.0 dynamic-slice_bitcast_fusion
  282.4 0.9 convolution_add_fusion
  283.3 0.9 copy_bitcast_fusion
  (161 shorter events, 35.5 us)
Async XLA Ops:
  10.0 6.0 %copy-start = (s32[512]{0:T(512)S(1)}, s32[512]{0:T(512)}, u32[]{:S(2)}) copy-start(s32[512]{0:T(512)} %param.13) | copy-start | bytes 6148
  10.0 55.7 %all-to-all-start = ((bf16[8,32,8192]{2,1,0:T(8,128)(2,1)}), bf16[8,32,8192]{2,1,0:T(8,128)(2,1)}, u32[]{:S(2)}, u32[]{:S(2)}) async-start(bf16[8,32,8192]{2,1,0:T(8,128)(2,1)} %stack.2), calls=%async_computation | async-start | bytes 8388608 | tf_op jit(solution)/shard_map/all_to_all | solution.py:34
  65.7 7.1 %copy-start.2 = (bf16[8192,256]{1,0:T(8,128)(2,1)S(1)}, bf16[8192,256]{1,0:T(8,128)(2,1)}, u32[]{:S(2)}) copy-start(bf16[8192,256]{1,0:T(8,128)(2,1)} %param.11) | copy-start | bytes 12582916
  77.2 38.3 %copy-start.1 = (s32[64]{0:T(128)S(1)}, s32[64]{0:T(128)}, u32[]{:S(2)}) copy-start(s32[64]{0:T(128)} %param.12) | copy-start | bytes 772
  79.8 34.5 %all-to-all-start.1 = ((bf16[32,16,768]{2,1,0:T(8,128)(2,1)}), bf16[32,16,768]{2,1,0:T(8,128)(2,1)S(1)}, u32[]{:S(2)}, u32[]{:S(2)}) async-start(bf16[32,16,768]{2,1,0:T(8,128)(2,1)} %scatter_fusion), calls=%async_computation.1 | async-start | bytes 1572864 | tf_op jit(solution)/shard_map/all_to_all | solution.py:45
  91.5 120.0 %all-gather.2.cloned.1.call-start = ((), (), s32[]{:S(2)}) async-start(), calls=%async_computation.2 | async-start | bytes 4325376 | tf_op jit(solution)/shard_map/all_gather | solution.py:66
Sparse Core Ops, SparseCore 0:
  115.7 95.8 all-gather.1
